TPU v7x, 32 devices: a whole 2x2x4 slice. The times are simulated.
32 devices in a mesh: row: 8 (over z, core), col: 4 (over y, x).
Axes of the slice: x: 2, y: 2, z: 4, core: 2. Of those that a mesh axis runs over, the one named last changes fastest.
Arguments:
- tokens: bfloat16 [12288, 2048], P('row', 'col'), may hold values from -6 to 6
- weight_query: bfloat16 [2048, 2048], P('row', 'col'), may hold values from -0.125 to 0.125
- weight_key: bfloat16 [2048, 2048], P('row', 'col'), may hold values from -0.125 to 0.125
- weight_value: bfloat16 [2048, 2048], P('row', 'col'), may hold values from -0.125 to 0.125
- weight_output: bfloat16 [2048, 2048], P('col', 'row'), may hold values from -0.125 to 0.125
- weight_gate: bfloat16 [2048, 8192], P('row', 'col'), may hold values from -0.125 to 0.125
- weight_up: bfloat16 [2048, 8192], P('row', 'col'), may hold values from -0.125 to 0.125
- weight_down: bfloat16 [8192, 2048], P('col', 'row'), may hold values from -0.0625 to 0.0625
- gain_query: float32 [2048], P('col'), may hold values from 0.25 to 1.75
- gain_key: float32 [2048], P('col'), may hold values from 0.25 to 1.75
- gain_attention: float32 [2048], replicated, may hold values from 0.5 to 1.5
- gain_feedforward: float32 [2048], replicated, may hold values from 0.5 to 1.5
- positions: int32 [12288], P('row'), may hold values from 0 to 1279, as said below
- segments: int32 [12288], P('row'), may hold values from 0 to 2, as said below
- cotangent: bfloat16 [12288, 2048], P('row', 'col'), may hold values from -6 to 6
Outputs:
- activations: bfloat16 [12288, 2048], P('row', 'col')
- input_grad: float32 [12288, 2048], P('row', 'col')
- query_weight_grad: float32 [2048, 2048], P('row', 'col')
- key_weight_grad: float32 [2048, 2048], P('row', 'col')
- value_weight_grad: float32 [2048, 2048], P('row', 'col')
- output_weight_grad: float32 [2048, 2048], P('col', 'row')
- gate_weight_grad: float32 [2048, 8192], P('row', 'col')
- up_weight_grad: float32 [2048, 8192], P('row', 'col')
- down_weight_grad: float32 [8192, 2048], P('col', 'row')
- query_gain_grad: float32 [2048], P('col')
- key_gain_grad: float32 [2048], P('col')
- attention_gain_grad: float32 [2048], replicated
- feedforward_gain_grad: float32 [2048], replicated
Inputs may be any that keep to these rules, and one draw needn't show every extreme that they name: The 1536 rows of each index of row form one group: the prompt's 1024 rows are consecutive with segment 0 and positions 0 to 1023; each continuation has 256 consecutive rows, one segment of 1 to 2 (each once a group) and positions 1024 to 1279 in order; the prompt lies before, between or after whole continuations. `segments`: segment ids of the layout described for positions.
All inputs are finite; a program needn't handle non-finite values.
Results may differ from a plain program's by a relative error of at most 0.02.
Values may be sent and summed in bfloat16 or wider, within the bound.
A program may use at most 320 MiB of HBM per device.

v0:
```python
import jax
import jax.numpy as jnp
from jax import lax
from jax.sharding import PartitionSpec as P

D = 2048
HD = 128
EPSILON = 1e-06
ROPE_BASE = 500000.0
NEGATIVE = -1e30
block_limit = 512


def times_plain(left, right):
    return jnp.dot(left, right, preferred_element_type=jnp.float32)


def times_transposed(left, right):
    return lax.dot_general(
        left, right, (((1,), (1,)), ((), ())), preferred_element_type=jnp.float32
    )


def transposed_times(left, right):
    return lax.dot_general(
        left, right, (((0,), (0,)), ((), ())), preferred_element_type=jnp.float32
    )


def rotation(positions):
    half_dim = HD // 2
    inverse = ROPE_BASE ** (-(jnp.arange(half_dim).astype(jnp.float32) * 2.0) / HD)
    angles = positions.astype(jnp.float32)[:, None] * inverse[None, :]
    return (jnp.cos(angles), jnp.sin(angles))


def rotate(values, cosine_table, sine_table, direction):
    row_count, local_width = values.shape
    local_heads = local_width // HD
    half_dim = HD // 2
    shaped = values.reshape(row_count, local_heads, HD)
    lower_half = shaped[..., :half_dim]
    upper_half = shaped[..., half_dim:]
    cosine_rows = cosine_table[:, None, :]
    sine_rows = direction * sine_table[:, None, :]
    rotated = jnp.concatenate(
        [
            lower_half * cosine_rows - upper_half * sine_rows,
            upper_half * cosine_rows + lower_half * sine_rows,
        ],
        axis=-1,
    )
    return rotated.reshape(row_count, local_width)


def allowed_pairs(segment_block, position_block, segments, positions):
    shared = (segments[None, :] == 0) | (segments[None, :] == segment_block[:, None])
    return shared & (positions[None, :] <= position_block[:, None])


def norm_back(incoming, values, norm_scale, gain_vector):
    scaled = gain_vector * incoming
    inner_mean = jnp.mean(scaled * values, axis=-1, keepdims=True)
    grad_values = norm_scale * scaled - values * norm_scale * norm_scale * norm_scale * inner_mean
    return (grad_values, jnp.sum(incoming * values * norm_scale, axis=0))


def spread_share(values, start):
    return lax.dynamic_update_slice_in_dim(jnp.zeros((D,), jnp.float32), values, start, 0)


def attend(query_rot, key_rot, value_low, segments, positions):
    row_count, local_width = query_rot.shape
    local_heads = local_width // HD
    block_rows = min(block_limit, row_count)
    blocks = row_count // block_rows
    key_heads = key_rot.reshape(row_count, local_heads, HD)
    value_heads = value_low.reshape(row_count, local_heads, HD)

    def one_block(packed):
        query_block, segment_block, position_block = packed
        query_heads = query_block.reshape(block_rows, local_heads, HD)
        scores = jnp.einsum(
            "qhd,khd->hqk", query_heads, key_heads, preferred_element_type=jnp.float32
        ) * HD ** (-0.5)
        allowed = allowed_pairs(segment_block, position_block, segments, positions)
        scores = jnp.where(allowed[None], scores, NEGATIVE)
        row_max = jnp.max(scores, axis=-1, keepdims=True)
        exponent = jnp.exp(scores - row_max)
        row_total = jnp.sum(exponent, axis=-1, keepdims=True)
        attn_probs = exponent / row_total
        context = jnp.einsum(
            "hqk,khd->qhd",
            attn_probs.astype(jnp.bfloat16),
            value_heads,
            preferred_element_type=jnp.float32,
        )
        return (context.reshape(block_rows, local_width), (row_max + jnp.log(row_total))[..., 0])

    context, log_norm = lax.map(
        one_block,
        (
            query_rot.reshape(blocks, block_rows, local_width),
            segments.reshape(blocks, block_rows),
            positions.reshape(blocks, block_rows),
        ),
    )
    return (context.reshape(row_count, local_width), log_norm)


def attend_back(query_rot, key_rot, value_low, context_grad, log_norm, segments, positions):
    row_count, local_width = query_rot.shape
    local_heads = local_width // HD
    block_rows = min(block_limit, row_count)
    blocks = row_count // block_rows
    scale_factor = HD ** (-0.5)
    key_heads = key_rot.reshape(row_count, local_heads, HD)
    value_heads = value_low.reshape(row_count, local_heads, HD)

    def one_block(carry, packed):
        key_total, value_total = carry
        query_block, grad_block, norm_block, segment_block, position_block = packed
        query_heads = query_block.reshape(block_rows, local_heads, HD)
        grad_heads = grad_block.reshape(block_rows, local_heads, HD)
        scores = (
            jnp.einsum("qhd,khd->hqk", query_heads, key_heads, preferred_element_type=jnp.float32)
            * scale_factor
        )
        allowed = allowed_pairs(segment_block, position_block, segments, positions)
        scores = jnp.where(allowed[None], scores, NEGATIVE)
        attn_probs = jnp.exp(scores - norm_block[..., None])
        prob_grad = jnp.einsum(
            "qhd,khd->hqk", grad_heads, value_heads, preferred_element_type=jnp.float32
        )
        delta_sum = jnp.sum(attn_probs * prob_grad, axis=-1, keepdims=True)
        score_grad = (attn_probs * (prob_grad - delta_sum)).astype(jnp.bfloat16)
        query_grad = (
            jnp.einsum("hqk,khd->qhd", score_grad, key_heads, preferred_element_type=jnp.float32)
            * scale_factor
        )
        key_total = (
            key_total
            + jnp.einsum(
                "hqk,qhd->khd", score_grad, query_heads, preferred_element_type=jnp.float32
            )
            * scale_factor
        )
        value_total = value_total + jnp.einsum(
            "hqk,qhd->khd",
            attn_probs.astype(jnp.bfloat16),
            grad_heads,
            preferred_element_type=jnp.float32,
        )
        return ((key_total, value_total), query_grad.reshape(block_rows, local_width))

    zeros_heads = jnp.zeros((row_count, local_heads, HD), jnp.float32)
    packed = (
        query_rot.reshape(blocks, block_rows, local_width),
        context_grad.reshape(blocks, block_rows, local_width),
        log_norm,
        segments.reshape(blocks, block_rows),
        positions.reshape(blocks, block_rows),
    )
    (key_grad, value_grad), query_grad = lax.scan(one_block, (zeros_heads, zeros_heads), packed)
    return (
        query_grad.reshape(row_count, local_width),
        key_grad.reshape(row_count, local_width),
        value_grad.reshape(row_count, local_width),
    )


def body(
    tokens,
    weight_query,
    weight_key,
    weight_value,
    weight_output,
    weight_gate,
    weight_up,
    weight_down,
    gain_query,
    gain_key,
    gain_attention,
    gain_feedforward,
    positions,
    segments,
    cotangent,
):
    col_width = tokens.shape[1]
    col_start = lax.axis_index("col") * col_width
    features = lax.all_gather(tokens, "col", axis=1, tiled=True)
    query_matrix, key_matrix, value_matrix, output_matrix, gate_matrix, up_matrix, down_matrix = (
        lax.all_gather(weight_query, "row", axis=0, tiled=True),
        lax.all_gather(weight_key, "row", axis=0, tiled=True),
        lax.all_gather(weight_value, "row", axis=0, tiled=True),
        lax.all_gather(weight_output, "row", axis=1, tiled=True),
        lax.all_gather(weight_gate, "row", axis=0, tiled=True),
        lax.all_gather(weight_up, "row", axis=0, tiled=True),
        lax.all_gather(weight_down, "row", axis=1, tiled=True),
    )
    query_raw = times_plain(features, query_matrix)
    key_raw = times_plain(features, key_matrix)
    value_low = times_plain(features, value_matrix).astype(jnp.bfloat16)
    square_sums = lax.psum(
        (jnp.sum(query_raw * query_raw, axis=-1), jnp.sum(key_raw * key_raw, axis=-1)), "col"
    )
    query_scale = lax.rsqrt(square_sums[0] / D + EPSILON)[:, None]
    key_scale = lax.rsqrt(square_sums[1] / D + EPSILON)[:, None]
    cosine_table, sine_table = rotation(positions)
    query_rot = rotate(query_raw * query_scale * gain_query, cosine_table, sine_table, 1.0).astype(
        jnp.bfloat16
    )
    key_rot = rotate(key_raw * key_scale * gain_key, cosine_table, sine_table, 1.0).astype(
        jnp.bfloat16
    )
    context, log_norm = attend(query_rot, key_rot, value_low, segments, positions)
    context_low = context.astype(jnp.bfloat16)
    attention_part = times_plain(context_low, output_matrix)
    attention_out = lax.psum(attention_part, "col")
    attention_scale = lax.rsqrt(
        jnp.mean(attention_out * attention_out, axis=-1, keepdims=True) + EPSILON
    )
    hidden_state = features.astype(jnp.float32) + attention_out * attention_scale * gain_attention
    hidden_low = hidden_state.astype(jnp.bfloat16)
    gate = times_plain(hidden_low, gate_matrix)
    up_rows = times_plain(hidden_low, up_matrix)
    sigmoid_gate = jax.nn.sigmoid(gate)
    silu_gate = gate * sigmoid_gate
    activated = (silu_gate * up_rows).astype(jnp.bfloat16)
    feedforward_part = times_plain(activated, down_matrix)
    feedforward_out = lax.psum(feedforward_part, "col")
    feedforward_scale = lax.rsqrt(
        jnp.mean(feedforward_out * feedforward_out, axis=-1, keepdims=True) + EPSILON
    )
    result = hidden_state + feedforward_out * feedforward_scale * gain_feedforward
    activations = lax.dynamic_slice_in_dim(result, col_start, col_width, 1).astype(jnp.bfloat16)
    upstream = lax.all_gather(cotangent, "col", axis=1, tiled=True).astype(jnp.float32)
    feedforward_full_grad, feedforward_gain_full = norm_back(
        upstream, feedforward_out, feedforward_scale, gain_feedforward
    )
    feedforward_gain_part = lax.dynamic_slice_in_dim(feedforward_gain_full, col_start, col_width, 0)
    feedforward_grad = feedforward_full_grad.astype(jnp.bfloat16)
    activated_grad = times_transposed(feedforward_grad, down_matrix)
    down_weight_grad = transposed_times(activated, feedforward_grad)
    gate_grad = (
        activated_grad * up_rows * sigmoid_gate * (1.0 + gate * (1.0 - sigmoid_gate))
    ).astype(jnp.bfloat16)
    up_grad = (activated_grad * silu_gate).astype(jnp.bfloat16)
    hidden_part = times_transposed(gate_grad, gate_matrix) + times_transposed(up_grad, up_matrix)
    gate_weight_grad = transposed_times(hidden_low, gate_grad)
    up_weight_grad = transposed_times(hidden_low, up_grad)
    hidden_grad = lax.psum(hidden_part, "col") + upstream
    attention_full_grad, attention_gain_full = norm_back(
        hidden_grad, attention_out, attention_scale, gain_attention
    )
    attention_gain_part = lax.dynamic_slice_in_dim(attention_gain_full, col_start, col_width, 0)
    attention_grad = attention_full_grad.astype(jnp.bfloat16)
    residual_grad = lax.dynamic_slice_in_dim(hidden_grad, col_start, col_width, 1)
    context_grad = times_transposed(attention_grad, output_matrix).astype(jnp.bfloat16)
    output_weight_grad = transposed_times(context_low, attention_grad)
    query_rot_grad, key_rot_grad, value_grad = attend_back(
        query_rot, key_rot, value_low, context_grad, log_norm, segments, positions
    )
    value_grad = value_grad.astype(jnp.bfloat16)
    query_norm_grad = rotate(query_rot_grad, cosine_table, sine_table, -1.0)
    key_norm_grad = rotate(key_rot_grad, cosine_table, sine_table, -1.0)
    query_scaled = gain_query * query_norm_grad
    key_scaled = gain_key * key_norm_grad
    inner_sums = lax.psum(
        (jnp.sum(query_scaled * query_raw, axis=-1), jnp.sum(key_scaled * key_raw, axis=-1)), "col"
    )
    query_raw_grad = (
        query_scale * query_scaled
        - query_raw * query_scale * query_scale * query_scale * (inner_sums[0] / D)[:, None]
    ).astype(jnp.bfloat16)
    key_raw_grad = (
        key_scale * key_scaled
        - key_raw * key_scale * key_scale * key_scale * (inner_sums[1] / D)[:, None]
    ).astype(jnp.bfloat16)
    query_gain_part = jnp.sum(query_norm_grad * query_raw * query_scale, axis=0)
    key_gain_part = jnp.sum(key_norm_grad * key_raw * key_scale, axis=0)
    input_part = (
        times_transposed(query_raw_grad, query_matrix)
        + times_transposed(key_raw_grad, key_matrix)
        + times_transposed(value_grad, value_matrix)
    )
    query_weight_part = transposed_times(features, query_raw_grad)
    key_weight_part = transposed_times(features, key_raw_grad)
    value_weight_part = transposed_times(features, value_grad)
    input_grad = (
        lax.psum_scatter(
            input_part.astype(jnp.bfloat16), "col", scatter_dimension=1, tiled=True
        ).astype(jnp.float32)
        + residual_grad
    )
    weight_grads = (
        lax.psum_scatter(
            query_weight_part.astype(jnp.bfloat16), "row", scatter_dimension=0, tiled=True
        ).astype(jnp.float32),
        lax.psum_scatter(
            key_weight_part.astype(jnp.bfloat16), "row", scatter_dimension=0, tiled=True
        ).astype(jnp.float32),
        lax.psum_scatter(
            value_weight_part.astype(jnp.bfloat16), "row", scatter_dimension=0, tiled=True
        ).astype(jnp.float32),
        lax.psum_scatter(
            output_weight_grad.astype(jnp.bfloat16), "row", scatter_dimension=1, tiled=True
        ).astype(jnp.float32),
        lax.psum_scatter(
            gate_weight_grad.astype(jnp.bfloat16), "row", scatter_dimension=0, tiled=True
        ).astype(jnp.float32),
        lax.psum_scatter(
            up_weight_grad.astype(jnp.bfloat16), "row", scatter_dimension=0, tiled=True
        ).astype(jnp.float32),
        lax.psum_scatter(
            down_weight_grad.astype(jnp.bfloat16), "row", scatter_dimension=1, tiled=True
        ).astype(jnp.float32),
    )
    gain_totals = lax.psum(
        (
            spread_share(query_gain_part, col_start),
            spread_share(key_gain_part, col_start),
            spread_share(attention_gain_part, col_start),
            spread_share(feedforward_gain_part, col_start),
        ),
        ("row", "col"),
    )
    query_gain_grad = lax.dynamic_slice_in_dim(gain_totals[0], col_start, col_width, 0)
    key_gain_grad = lax.dynamic_slice_in_dim(gain_totals[1], col_start, col_width, 0)
    return (
        activations,
        input_grad,
        weight_grads[0],
        weight_grads[1],
        weight_grads[2],
        weight_grads[3],
        weight_grads[4],
        weight_grads[5],
        weight_grads[6],
        query_gain_grad,
        key_gain_grad,
        gain_totals[2],
        gain_totals[3],
    )


def solution(mesh):
    in_specs = (
        P("row", "col"),
        P("row", "col"),
        P("row", "col"),
        P("row", "col"),
        P("col", "row"),
        P("row", "col"),
        P("row", "col"),
        P("col", "row"),
        P("col"),
        P("col"),
        P(),
        P(),
        P("row"),
        P("row"),
        P("row", "col"),
    )
    out_specs = (
        P("row", "col"),
        P("row", "col"),
        P("row", "col"),
        P("row", "col"),
        P("row", "col"),
        P("col", "row"),
        P("row", "col"),
        P("row", "col"),
        P("col", "row"),
        P("col"),
        P("col"),
        P(),
        P(),
    )
    return jax.shard_map(body, mesh=mesh, in_specs=in_specs, out_specs=out_specs, check_vma=False)
```

profile of v0, /device:TPU:0, one launch (start us, length us, event | category | flops | bytes accessed | tf_op | source)
XLA Modules:
  0.0 2133.4 jit_solution(11342082336165431979)
XLA Ops:
  17.7 23.7 %all-gather.12.cloned.1.call-done = bf16[2048,512]{1,0:T(8,128)(2,1)} async-done(((bf16[256,512]{1,0:T(8,128)(2,1)}), bf16[2048,512]{1,0:T(8,128)(2,1)}) %all-gather.12.cloned.1.call-update) | async-done | bytes 2097168 | tf_op jit(solution)/shard_map/all_gather | solution.py:193
  41.5 71.2 %all-gather.10.cloned.1.call-done = bf16[1536,2048]{1,0:T(8,128)(2,1)} async-done(((bf16[1536,512]{1,0:T(8,128)(2,1)}), bf16[1536,2048]{1,0:T(8,128)(2,1)}) %all-gather.10.cloned.1.call-update) | async-done | bytes 6291472 | tf_op jit(solution)/shard_map/all_gather | solution.py:191
  119.0 24.5 %all-gather.14.cloned.1.call-done = bf16[2048,512]{1,0:T(8,128)(2,1)} async-done(((bf16[256,512]{1,0:T(8,128)(2,1)}), bf16[2048,512]{1,0:T(8,128)(2,1)}) %all-gather.14.cloned.1.call-update) | async-done | bytes 2097168 | tf_op jit(solution)/shard_map/all_gather | solution.py:194
  152.0 16.2 all-reduce.2
  211.1 47.7 %while.29 = (s32[]{:T(128)}, bf16[3,512,512]{2,1,0:T(8,128)(2,1)}, f32[3,4,512]{2,1,0:T(4,128)}, s32[1536]{0:T(1024)S(1)}, s32[3,512]{1,0:T(4,128)S(1)}, /*index...) while((s32[]{:T(128)}, bf16[3,512,512]{2,1,0:T(8,128)(2,1)}, ...), condition=%wide.region_7.8_spmd.clone, body=%wide.region_4.7_spmd.sunk.clone | while | flops 1651506688 | bytes 54626440 | solution.py:100
  271.3 234.8 %all-reduce.7.cloned.1.call-done = f32[1536,2048]{1,0:T(8,128)} async-done(((f32[1536,2048]{1,0:T(8,128)}), f32[1536,2048]{1,0:T(8,128)}) %all-reduce.7.cloned.1.call-update) | async-done | bytes 12582928 | tf_op jit(solution)/shard_map/psum | solution.py:219
  514.3 10.6 fusion.31
  524.9 64.8 %all-gather.20.cloned.1.call-done = bf16[2048,2048]{1,0:T(8,128)(2,1)} async-done(((bf16[256,2048]{1,0:T(8,128)(2,1)}), bf16[2048,2048]{1,0:T(8,128)(2,1)}) %all-gather.20.cloned.1.call-update) | async-done | bytes 8388624 | tf_op jit(solution)/shard_map/all_gather | solution.py:197
  589.8 19.0 fusion.36
  608.7 63.2 %all-gather.22.cloned.1.call-done = bf16[2048,2048]{1,0:T(8,128)(2,1)} async-done(((bf16[256,2048]{1,0:T(8,128)(2,1)}), bf16[2048,2048]{1,0:T(8,128)(2,1)}) %all-gather.22.cloned.1.call-update) | async-done | bytes 8388624 | tf_op jit(solution)/shard_map/all_gather | solution.py:198
  671.9 23.5 %multiply_convert_fusion.3 = (bf16[1536,2048]{1,0:T(8,128)(2,1)}, f32[1536,2048]{1,0:T(8,128)}) fusion(f32[1536,2048]{1,0:T(8,128)} %fusion.36, bf16[1536,2048]{1,0:T(8,128)(2,1)} %get-tuple-element.317, bf16[2048,2048]{1,0:T(8,128)(2,1)} %all-gather.22.cloned.1.call-done), kind=kOutput, calls=%fused_computation.51 | convolution fusion | flops 12903776256 | bytes 46137344 | tf_op jit(solution)/shard_map/dot_general | solution.py:15
  695.5 59.0 %all-gather.24.cloned.1.call-done = bf16[2048,2048]{1,0:T(8,128)(2,1)} async-done(((bf16[2048,256]{1,0:T(8,128)(2,1)}), bf16[2048,2048]{1,0:T(8,128)(2,1)}) %all-gather.24.cloned.1.call-update) | async-done | bytes 8388624 | tf_op jit(solution)/shard_map/all_gather | solution.py:199
  754.5 18.9 fusion.37
  774.4 236.7 %all-reduce.9.cloned.1.call-done = f32[1536,2048]{1,0:T(8,128)} async-done(((f32[1536,2048]{1,0:T(8,128)}), f32[1536,2048]{1,0:T(8,128)}) %all-reduce.9.cloned.1.call-update) | async-done | bytes 12582928 | tf_op jit(solution)/shard_map/psum | solution.py:231
  1016.5 66.3 %all-gather.26.cloned.1.call-done = bf16[1536,2048]{1,0:T(8,128)(2,1)} async-done(((bf16[1536,512]{1,0:T(8,128)(2,1)}), bf16[1536,2048]{1,0:T(8,128)(2,1)}) %all-gather.26.cloned.1.call-update) | async-done | bytes 6291472 | tf_op jit(solution)/shard_map/all_gather | solution.py:237
  1102.5 26.6 %multiply_convert_fusion.1 = (bf16[1536,2048]{1,0:T(8,128)(2,1)}, bf16[1536,2048]{1,0:T(8,128)(2,1)}) fusion(f32[1536,2048]{1,0:T(8,128)} %fusion.36, f32[1536,2048]{1,0:T(8,128)} %get-tuple-element.355, bf16[1536,2048]{1,0:T(8,128)(2,1)} %get-tuple-element.329, bf16[2048,2048]{1,0:T(8,128)(2,1)} %all-gather.24.cloned.1.call-done), kind=kOutput, calls=%fused_computation.48 | convolution fusion | flops 12925796352 | bytes 52428800 | tf_op jit(solution)/shard_map/dot_general | solution.py:19
  1129.2 19.2 fusion.38
  1148.4 20.7 convolution_add_fusion
  1173.6 234.9 %all-reduce.11.cloned.1.call-done = f32[1536,2048]{1,0:T(8,128)} async-done(((f32[1536,2048]{1,0:T(8,128)}), f32[1536,2048]{1,0:T(8,128)}) %all-reduce.11.cloned.1.call-update) | async-done | bytes 12582928 | tf_op jit(solution)/shard_map/psum | solution.py:252
  1408.5 12.4 multiply_reduce_fusion.1
  1436.2 127.1 %while.30 = (s32[]{:T(128)}, f32[1536,4,128]{0,2,1:T(8,128)}, f32[1536,4,128]{0,2,1:T(8,128)}, f32[3,512,512]{2,1,0:T(8,128)}, bf16[3,512,512]{1,2,0:T(8,128)(2,...) while((s32[]{:T(128)}, f32[1536,4,128]{0,2,1:T(8,128)}, ...), condition=%wide.region_17.18_spmd.clone.clone, body=%wide.region_15.17_spmd.clone.sunk.clone | while | flops 4062182912 | bytes 245442384 | solution.py:164
  1603.6 15.1 all-reduce.1
  1631.1 19.6 convolution_convert_fusion
  1670.6 20.3 convolution_convert_fusion.2
  1691.0 20.0 convolution_convert_fusion.1
  1736.9 13.3 add_convert_fusion
  1758.0 41.1 %all-reduce = (f32[2048]{0:T(1024)S(1)}, f32[2048]{0:T(1024)S(1)}, f32[2048]{0:T(1024)}, f32[2048]{0:T(1024)}) all-reduce(f32[2048]{0:T(1024)S(1)} %dynamic_update_slice.23, f32[2048]{0:T(1024)S(1)} %dynamic_update_slice.24, f32[2048]{0:T(1024)S(1)} %dynamic-slice_dynamic-update-slice_fusion.1, ...), channel_id=1, replica_groups=mesh['row'=8,'col'=4] {'row','col'}, use_global_device_ids=true, to_apply=%region_31.32 | all-reduce | flops 8192 | bytes 65536 | tf_op jit(solution)/shard_map/psum | solution.py:319
  1806.8 25.9 %reduce-scatter.11.cloned.1.call-done = bf16[256,512]{0,1:T(8,128)(2,1)} async-done(((bf16[2048,512]{0,1:T(8,128)(2,1)}), bf16[256,512]{0,1:T(8,128)(2,1)}) %reduce-scatter.11.cloned.1.call-update) | async-done | bytes 262160 | tf_op jit(solution)/shard_map/reduce_scatter | solution.py:297
  1834.5 88.3 %reduce-scatter.19.cloned.1.call-done = bf16[256,2048]{1,0:T(8,128)(2,1)} async-done(((bf16[2048,2048]{1,0:T(8,128)(2,1)}), bf16[256,2048]{1,0:T(8,128)(2,1)}) %reduce-scatter.19.cloned.1.call-update) | async-done | bytes 1048592 | tf_op jit(solution)/shard_map/reduce_scatter | solution.py:309
  1925.6 87.4 %reduce-scatter.21.cloned.1.call-done = bf16[256,2048]{1,0:T(8,128)(2,1)} async-done(((bf16[2048,2048]{1,0:T(8,128)(2,1)}), bf16[256,2048]{1,0:T(8,128)(2,1)}) %reduce-scatter.21.cloned.1.call-update) | async-done | bytes 1048592 | tf_op jit(solution)/shard_map/reduce_scatter | solution.py:312
  2015.8 34.6 %reduce-scatter.15.cloned.1.call-done = bf16[256,512]{0,1:T(8,128)(2,1)} async-done(((bf16[2048,512]{0,1:T(8,128)(2,1)}), bf16[256,512]{0,1:T(8,128)(2,1)}) %reduce-scatter.15.cloned.1.call-update) | async-done | bytes 262160 | tf_op jit(solution)/shard_map/reduce_scatter | solution.py:303
  2052.3 69.5 %reduce-scatter.9.cloned.1.call-done = bf16[1536,512]{1,0:T(8,128)(2,1)} async-done(((bf16[1536,2048]{1,0:T(8,128)(2,1)}), bf16[1536,512]{1,0:T(8,128)(2,1)}) %reduce-scatter.9.cloned.1.call-update) | async-done | bytes 1572880 | tf_op jit(solution)/shard_map/reduce_scatter | solution.py:291
  (333 shorter events, 436.0 us)
Async XLA Ops:
  7.2 34.3 %all-gather.12.cloned.1.call-start = ((), (), s32[]{:S(2)}) async-start(), calls=%async_computation.9 | async-start | bytes 2359296 | tf_op jit(solution)/shard_map/all_gather | solution.py:193
  7.9 104.7 %all-gather.10.cloned.1.call-start = ((), (), s32[]{:S(2)}) async-start(), calls=%async_computation.8 | async-start | bytes 7864320 | tf_op jit(solution)/shard_map/all_gather | solution.py:191
  8.7 134.8 %all-gather.14.cloned.1.call-start = ((), (), s32[]{:S(2)}) async-start(), calls=%async_computation.10 | async-start | bytes 2359296 | tf_op jit(solution)/shard_map/all_gather | solution.py:194
  9.4 193.6 %all-gather.16.cloned.1.call-start = ((), (), s32[]{:S(2)}) async-start(), calls=%async_computation.11 | async-start | bytes 2359296 | tf_op jit(solution)/shard_map/all_gather | solution.py:195
  10.0 248.9 %all-gather.18.cloned.1.call-start = ((), (), s32[]{:S(2)}) async-start(), calls=%async_computation.12 | async-start | bytes 2359296 | tf_op jit(solution)/shard_map/all_gather | solution.py:196
  10.6 495.5 %all-reduce.7.cloned.1.call-start = ((), (), s32[]{:S(2)}) async-start(), calls=%async_computation.13 | async-start | bytes 25165824 | tf_op jit(solution)/shard_map/psum | solution.py:219
  119.0 49.3 %copy-start.11 = (f32[1536,512]{0,1:T(8,128)}, f32[1536,512]{0,1:T(8,128)S(1)}, u32[]{:S(2)}) copy-start(f32[1536,512]{0,1:T(8,128)S(1)} %get-tuple-element.351) | copy-start | bytes 9437188
  119.0 49.3 %copy-start.47 = (f32[512]{0:T(512)S(1)}, f32[512]{0:T(512)}, u32[]{:S(2)}) copy-start(f32[512]{0:T(512)} %param.27) | copy-start | bytes 6148
  258.9 10.1 copy-start.41
  269.0 320.8 %all-gather.20.cloned.1.call-start = ((), (), s32[]{:S(2)}) async-start(), calls=%async_computation.14 | async-start | bytes 9437184 | tf_op jit(solution)/shard_map/all_gather | solution.py:197
  269.7 402.2 %all-gather.22.cloned.1.call-start = ((), (), s32[]{:S(2)}) async-start(), calls=%async_computation.15 | async-start | bytes 9437184 | tf_op jit(solution)/shard_map/all_gather | solution.py:198
  270.5 484.0 %all-gather.24.cloned.1.call-start = ((), (), s32[]{:S(2)}) async-start(), calls=%async_computation.16 | async-start | bytes 9437184 | tf_op jit(solution)/shard_map/all_gather | solution.py:199
  271.2 241.1 %copy-start.42 = (f32[2048]{0:T(1024)S(1)}, f32[2048]{0:T(1024)}, u32[]{:S(2)}) copy-start(f32[2048]{0:T(1024)} %param.29) | copy-start | bytes 24580
  271.2 739.8 %all-reduce.9.cloned.1.call-start = ((), (), s32[]{:S(2)}) async-start(), calls=%async_computation.17 | async-start | bytes 25165824 | tf_op jit(solution)/shard_map/psum | solution.py:231
  773.4 309.4 %all-gather.26.cloned.1.call-start = ((), (), s32[]{:S(2)}) async-start(), calls=%async_computation.18 | async-start | bytes 7864320 | tf_op jit(solution)/shard_map/all_gather | solution.py:237
  774.2 308.6 %copy-start.44 = (f32[2048]{0:T(1024)S(1)}, f32[2048]{0:T(1024)}, u32[]{:S(2)}) copy-start(f32[2048]{0:T(1024)} %param.30) | copy-start | bytes 24580
  774.2 634.3 %all-reduce.11.cloned.1.call-start = ((), (), s32[]{:S(2)}) async-start(), calls=%async_computation.19 | async-start | bytes 25165824 | tf_op jit(solution)/shard_map/psum | solution.py:252
  1082.8 10.2 copy-start.6
  1082.8 11.8 copy-start.10
  1129.2 19.2 copy-start.51
  1169.1 631.3 %reduce-scatter.13.cloned.1.call-start = ((), (), s32[]{:S(2)}) async-start(), calls=%async_computation.22 | async-start | bytes 2359296 | tf_op jit(solution)/shard_map/reduce_scatter | solution.py:300
  1170.5 238.1 %copy-start.39 = (f32[1536]{0:T(1024)S(1)}, f32[1536]{0:T(1024)}, u32[]{:S(2)}) copy-start(f32[1536]{0:T(1024)} %copy-done.38) | copy-start | bytes 18436
  1170.5 238.1 %copy-start.43 = (f32[2048]{0:T(1024)S(1)}, f32[2048]{0:T(1024)}, u32[]{:S(2)}) copy-start(f32[2048]{0:T(1024)} %param.29) | copy-start | bytes 24580
  1421.0 10.6 copy-start.8
  1421.0 10.6 copy-start.50
  1631.1 171.2 %reduce-scatter.23.cloned.1.call-start = ((), (), s32[]{:S(2)}) async-start(), calls=%async_computation.27 | async-start | bytes 9437184 | tf_op jit(solution)/shard_map/reduce_scatter | solution.py:315
  1650.8 154.2 %reduce-scatter.17.cloned.1.call-start = ((), (), s32[]{:S(2)}) async-start(), calls=%async_computation.24 | async-start | bytes 2359296 | tf_op jit(solution)/shard_map/reduce_scatter | solution.py:306
  1659.0 173.6 %reduce-scatter.11.cloned.1.call-start = ((), (), s32[]{:S(2)}) async-start(), calls=%async_computation.21 | async-start | bytes 2359296 | tf_op jit(solution)/shard_map/reduce_scatter | solution.py:297
  1670.6 252.3 %reduce-scatter.19.cloned.1.call-start = ((), (), s32[]{:S(2)}) async-start(), calls=%async_computation.25 | async-start | bytes 9437184 | tf_op jit(solution)/shard_map/reduce_scatter | solution.py:309
  1691.0 322.0 %reduce-scatter.21.cloned.1.call-start = ((), (), s32[]{:S(2)}) async-start(), calls=%async_computation.26 | async-start | bytes 9437184 | tf_op jit(solution)/shard_map/reduce_scatter | solution.py:312
  1711.0 339.4 %reduce-scatter.15.cloned.1.call-start = ((), (), s32[]{:S(2)}) async-start(), calls=%async_computation.23 | async-start | bytes 2359296 | tf_op jit(solution)/shard_map/reduce_scatter | solution.py:303
  1721.8 400.0 %reduce-scatter.9.cloned.1.call-start = ((), (), s32[]{:S(2)}) async-start(), calls=%async_computation.20 | async-start | bytes 7864320 | tf_op jit(solution)/shard_map/reduce_scatter | solution.py:291
  (54 other events, 271.3 us)
Sparse Core Ops, SparseCore 0:
  9.6 31.8 all-gather.11
  43.3 69.3 all-gather.9
  114.3 29.1 all-gather.13
  144.9 28.5 all-gather.15
  174.9 30.0 all-gather.17
  269.1 236.9 all-reduce.6
  507.7 82.0 all-gather.19
  591.4 80.5 all-gather.21
  673.5 80.9 all-gather.23
  773.6 237.4 all-reduce.8
  1012.9 69.8 all-gather.25
  1169.2 239.2 all-reduce.10
  1631.2 36.1 reduce-scatter.12
  1669.5 87.8 reduce-scatter.22
  1760.1 34.8 reduce-scatter.16
  1797.7 34.8 reduce-scatter.10
  1834.8 88.0 reduce-scatter.18
  1925.0 87.9 reduce-scatter.20
  2015.9 34.5 reduce-scatter.14
  2053.3 68.5 reduce-scatter.8
where the time goes:
time: 2140 us; the launch traced here: 2130 us
  waiting for transfers between devices  1390 us (65%)
  matrix products  384 us (18%)
  other arithmetic  160 us (7%)
  local copies, waits for them, and re-layouts  109 us (5%)
  blocking collectives  72.4 us (3%)
    psum x1, waiting for transfers between devices, body(): feedforward_out = lax.psum(feedforward_part, 'col')  237 us
    psum x1, waiting for transfers between devices, body(): hidden_grad = lax.psum(hidden_part, 'col') + upstream  235 us
    psum x1, waiting for transfers between devices, body(): attention_out = lax.psum(attention_part, 'col')  235 us
    dot_general x7, matrix products, times_transposed(): lax.dot_general(left, right, (((1,), (1,)), ((), ())), preferred_element_...  99.4 us
    dot_general x7, matrix products, times_plain(): return jnp.dot(left, right, preferred_element_type=jnp.float32)  94.4 us
    dot_general x7, matrix products, transposed_times(): lax.dot_general(left, right, (((0,), (0,)), ((), ())), preferred_element_...  90.8 us
    reduce_scatter x1, waiting for transfers between devices, body(): lax.psum_scatter(gate_weight_grad.astype(jnp.bfloat16), 'row', scatter_di...  88.3 us
    reduce_scatter x1, waiting for transfers between devices, body(): lax.psum_scatter(up_weight_grad.astype(jnp.bfloat16), 'row', scatter_dime...  87.4 us
  transfers between devices with their start and end apart: 20, of which 15 were waited for; matrix products, arithmetic and copies ran while one was open for 15% of the time, Pallas kernels for 0%

commit v1 on v0

--- a/solution.py
+++ b/solution.py
@@ -188,7 +188,16 @@
 ):
     col_width = tokens.shape[1]
     col_start = lax.axis_index("col") * col_width
-    features = lax.all_gather(tokens, "col", axis=1, tiled=True)
+    ways = lax.axis_size("col")
+    up = [(d, (d + 1) % ways) for d in range(ways)]
+    down = [(d, (d - 1) % ways) for d in range(ways)]
+    earlier, later = ([tokens], [tokens])
+    for _ in range(ways // 2):
+        earlier.append(lax.ppermute(earlier[-1], "col", up))
+    for _ in range((ways - 1) // 2):
+        later.append(lax.ppermute(later[-1], "col", down))
+    line = jnp.concatenate([*earlier[::-1], *later[1:]], axis=1)
+    features = jnp.roll(line, (lax.axis_index("col") - ways // 2) * tokens.shape[1], axis=1)
     query_matrix, key_matrix, value_matrix, output_matrix, gate_matrix, up_matrix, down_matrix = (
         lax.all_gather(weight_query, "row", axis=0, tiled=True),
         lax.all_gather(weight_key, "row", axis=0, tiled=True),

time: 2140 us -> 2130 us (level)
  waiting for transfers between devices: 1390 us -> 1360 us
    ppermute x0 -> x3, waiting for transfers between devices: none -> 89.5 us  [the longest x2 63 us: body(): earlier.append(lax.ppermute(earlier[-1], 'col', up))]
    reduce_scatter x1, waiting for transfers between devices: 0.01 us -> 87.4 us  [body(): lax.psum_scatter(down_weight_grad.astype(jnp.bfloat16), 'row', scatter_di...]
    all_gather x1 -> x0, waiting for transfers between devices: 71.2 us -> none  [body(): features = lax.all_gather(tokens, 'col', axis=1, tiled=True)]
    reduce_scatter x1, waiting for transfers between devices: 34.6 us -> 0.01 us  [body(): lax.psum_scatter(value_weight_part.astype(jnp.bfloat16), 'row', scatter_d...]
    reduce_scatter x1, waiting for transfers between devices: 25.9 us -> 0.01 us  [body(): lax.psum_scatter(query_weight_part.astype(jnp.bfloat16), 'row', scatter_d...]
    all_gather x1, waiting for transfers between devices: 24.5 us -> 0.01 us  [body(): lax.all_gather(weight_key, 'row', axis=0, tiled=True)]
    reduce_scatter x1, waiting for transfers between devices: 88.3 us -> 64.3 us  [body(): lax.psum_scatter(gate_weight_grad.astype(jnp.bfloat16), 'row', scatter_di...]
    all_gather x1, waiting for transfers between devices: 23.7 us -> 0.02 us  [body(): lax.all_gather(weight_query, 'row', axis=0, tiled=True)]
  transfers between devices with their start and end apart: 20 -> 22, of which waited for: 15 -> 14; matrix products, arithmetic and copies ran while one was open for 15% -> 16% of each run, Pallas kernels for 0% -> 0%
where the time goes in v1:
time: 2130 us; the launch traced here: 2120 us
  waiting for transfers between devices  1360 us (64%)
  matrix products  375 us (18%)
  other arithmetic  169 us (8%)
  local copies, waits for them, and re-layouts  118 us (6%)
  blocking collectives  69.8 us (3%)
    psum x1, waiting for transfers between devices, body(): attention_out = lax.psum(attention_part, 'col')  238 us
    psum x1, waiting for transfers between devices, body(): feedforward_out = lax.psum(feedforward_part, 'col')  237 us
    psum x1, waiting for transfers between devices, body(): hidden_grad = lax.psum(hidden_part, 'col') + upstream  235 us
    dot_general x7, matrix products, times_transposed(): lax.dot_general(left, right, (((1,), (1,)), ((), ())), preferred_element_...  99.1 us
    dot_general x7, matrix products, times_plain(): return jnp.dot(left, right, preferred_element_type=jnp.float32)  95.6 us
    dot_general x7, matrix products, transposed_times(): lax.dot_general(left, right, (((0,), (0,)), ((), ())), preferred_element_...  90 us
    reduce_scatter x1, waiting for transfers between devices, body(): lax.psum_scatter(down_weight_grad.astype(jnp.bfloat16), 'row', scatter_di...  87.4 us
    reduce_scatter x1, waiting for transfers between devices, body(): lax.psum_scatter(up_weight_grad.astype(jnp.bfloat16), 'row', scatter_dime...  87.4 us
  transfers between devices with their start and end apart: 22, of which 14 were waited for; matrix products, arithmetic and copies ran while one was open for 16% of the time, Pallas kernels for 0%

profile of v1, /device:TPU:0, one launch (start us, length us, event | category | flops | bytes accessed | tf_op | source)
XLA Modules:
  0.0 2119.6 jit_solution(6939797391300652439)
XLA Ops:
  12.5 35.6 %collective-permute-done = bf16[1536,512]{1,0:T(8,128)(2,1)S(1)} collective-permute-done((bf16[1536,512]{1,0:T(8,128)(2,1)}, bf16[1536,512]{1,0:T(8,128)(2,1)S(1)}, u32[]{:S(2)}, u32[]{:S(2)}) %collective-permute-start) | collective-permute-done | bytes 1572896 | tf_op jit(solution)/shard_map/ppermute | solution.py:196
  58.8 27.5 %collective-permute-done.1 = bf16[1536,512]{1,0:T(8,128)(2,1)} collective-permute-done((bf16[1536,512]{1,0:T(8,128)(2,1)S(1)}, bf16[1536,512]{1,0:T(8,128)(2,1)}, u32[]{:S(2)}, u32[]{:S(2)}) %collective-permute-start.1) | collective-permute-done | bytes 1572896 | tf_op jit(solution)/shard_map/ppermute | solution.py:196
  91.7 26.5 %collective-permute-done.2 = bf16[1536,512]{1,0:T(8,128)(2,1)S(1)} collective-permute-done((bf16[1536,512]{1,0:T(8,128)(2,1)}, bf16[1536,512]{1,0:T(8,128)(2,1)S(1)}, u32[]{:S(2)}, u32[]{:S(2)}) %collective-permute-start.2) | collective-permute-done | bytes 1572896 | tf_op jit(solution)/shard_map/ppermute | solution.py:198
  142.2 14.5 all-reduce.2
  203.5 47.8 %while.29 = (s32[]{:T(128)}, bf16[3,512,512]{2,1,0:T(8,128)(2,1)}, f32[3,4,512]{2,1,0:T(4,128)}, s32[1536]{0:T(1024)S(1)}, s32[3,512]{1,0:T(4,128)S(1)}, /*index...) while((s32[]{:T(128)}, bf16[3,512,512]{2,1,0:T(8,128)(2,1)}, ...), condition=%wide.region_7.8_spmd.clone, body=%wide.region_4.7_spmd.sunk.clone | while | flops 1651506688 | bytes 54625432 | solution.py:100
  263.6 237.6 %all-reduce.7.cloned.1.call-done = f32[1536,2048]{1,0:T(8,128)} async-done(((f32[1536,2048]{1,0:T(8,128)}), f32[1536,2048]{1,0:T(8,128)}) %all-reduce.7.cloned.1.call-update) | async-done | bytes 12582928 | tf_op jit(solution)/shard_map/psum | solution.py:228
  509.5 10.4 fusion.42
  519.9 64.8 %all-gather.17.cloned.1.call-done = bf16[2048,2048]{1,0:T(8,128)(2,1)} async-done(((bf16[256,2048]{1,0:T(8,128)(2,1)}), bf16[2048,2048]{1,0:T(8,128)(2,1)}) %all-gather.17.cloned.1.call-update) | async-done | bytes 8388624 | tf_op jit(solution)/shard_map/all_gather | solution.py:206
  584.7 18.9 fusion.47
  603.6 63.3 %all-gather.19.cloned.1.call-done = bf16[2048,2048]{1,0:T(8,128)(2,1)} async-done(((bf16[256,2048]{1,0:T(8,128)(2,1)}), bf16[2048,2048]{1,0:T(8,128)(2,1)}) %all-gather.19.cloned.1.call-update) | async-done | bytes 8388624 | tf_op jit(solution)/shard_map/all_gather | solution.py:207
  666.9 23.7 %multiply_convert_fusion.3 = (bf16[1536,2048]{1,0:T(8,128)(2,1)}, f32[1536,2048]{1,0:T(8,128)}) fusion(f32[1536,2048]{1,0:T(8,128)} %fusion.47, bf16[1536,2048]{1,0:T(8,128)(2,1)} %get-tuple-element.291, bf16[2048,2048]{1,0:T(8,128)(2,1)} %all-gather.19.cloned.1.call-done), kind=kOutput, calls=%fused_computation.51 | convolution fusion | flops 12903776256 | bytes 46137344 | tf_op jit(solution)/shard_map/dot_general | solution.py:15
  690.6 58.9 %all-gather.21.cloned.1.call-done = bf16[2048,2048]{1,0:T(8,128)(2,1)} async-done(((bf16[2048,256]{1,0:T(8,128)(2,1)}), bf16[2048,2048]{1,0:T(8,128)(2,1)}) %all-gather.21.cloned.1.call-update) | async-done | bytes 8388624 | tf_op jit(solution)/shard_map/all_gather | solution.py:208
  749.5 18.9 fusion.48
  769.2 236.8 %all-reduce.9.cloned.1.call-done = f32[1536,2048]{1,0:T(8,128)} async-done(((f32[1536,2048]{1,0:T(8,128)}), f32[1536,2048]{1,0:T(8,128)}) %all-reduce.9.cloned.1.call-update) | async-done | bytes 12582928 | tf_op jit(solution)/shard_map/psum | solution.py:240
  1011.5 66.1 %all-gather.23.cloned.1.call-done = bf16[1536,2048]{1,0:T(8,128)(2,1)} async-done(((bf16[1536,512]{1,0:T(8,128)(2,1)}), bf16[1536,2048]{1,0:T(8,128)(2,1)}) %all-gather.23.cloned.1.call-update) | async-done | bytes 6291472 | tf_op jit(solution)/shard_map/all_gather | solution.py:246
  1097.5 26.5 %multiply_convert_fusion.1 = (bf16[1536,2048]{1,0:T(8,128)(2,1)}, bf16[1536,2048]{1,0:T(8,128)(2,1)}) fusion(f32[1536,2048]{1,0:T(8,128)} %fusion.47, f32[1536,2048]{1,0:T(8,128)} %get-tuple-element.329, bf16[1536,2048]{1,0:T(8,128)(2,1)} %get-tuple-element.303, bf16[2048,2048]{1,0:T(8,128)(2,1)} %all-gather.21.cloned.1.call-done), kind=kOutput, calls=%fused_computation.48 | convolution fusion | flops 12925796352 | bytes 52428800 | tf_op jit(solution)/shard_map/dot_general | solution.py:19
  1124.0 19.2 fusion.49
  1143.2 20.6 convolution_add_fusion
  1168.3 234.9 %all-reduce.11.cloned.1.call-done = f32[1536,2048]{1,0:T(8,128)} async-done(((f32[1536,2048]{1,0:T(8,128)}), f32[1536,2048]{1,0:T(8,128)}) %all-reduce.11.cloned.1.call-update) | async-done | bytes 12582928 | tf_op jit(solution)/shard_map/psum | solution.py:261
  1403.3 12.4 multiply_reduce_fusion.1
  1415.7 10.6 subtract_convert_fusion
  1431.0 119.3 %while.30 = (s32[]{:T(128)}, f32[1536,4,128]{0,2,1:T(8,128)}, f32[1536,4,128]{0,2,1:T(8,128)}, f32[3,512,512]{2,1,0:T(8,128)}, bf16[3,512,512]{1,2,0:T(8,128)(2,...) while((s32[]{:T(128)}, f32[1536,4,128]{0,2,1:T(8,128)}, ...), condition=%wide.region_17.18_spmd.clone.clone, body=%wide.region_15.17_spmd.clone.sunk.clone | while | flops 4062182912 | bytes 262219120 | solution.py:164
  1590.3 15.1 all-reduce.1
  1647.0 19.4 convolution_convert_fusion.2
  1666.4 19.6 convolution_convert_fusion.1
  1686.2 19.9 convolution_convert_fusion
  1722.5 13.2 add_convert_fusion
  1743.5 40.2 %all-reduce = (f32[2048]{0:T(1024)S(1)}, f32[2048]{0:T(1024)S(1)}, f32[2048]{0:T(1024)}, f32[2048]{0:T(1024)}) all-reduce(f32[2048]{0:T(1024)S(1)} %dynamic_update_slice.23, f32[2048]{0:T(1024)S(1)} %dynamic_update_slice.24, f32[2048]{0:T(1024)S(1)} %dynamic-slice_dynamic-update-slice_fusion.1, ...), channel_id=1, replica_groups=mesh['row'=8,'col'=4] {'row','col'}, use_global_device_ids=true, to_apply=%region_31.32 | all-reduce | flops 8192 | bytes 65536 | tf_op jit(solution)/shard_map/psum | solution.py:328
  1792.2 64.3 %reduce-scatter.19.cloned.1.call-done = bf16[256,2048]{1,0:T(8,128)(2,1)} async-done(((bf16[2048,2048]{1,0:T(8,128)(2,1)}), bf16[256,2048]{1,0:T(8,128)(2,1)}) %reduce-scatter.19.cloned.1.call-update) | async-done | bytes 1048592 | tf_op jit(solution)/shard_map/reduce_scatter | solution.py:318
  1859.3 87.4 %reduce-scatter.21.cloned.1.call-done = bf16[256,2048]{1,0:T(8,128)(2,1)} async-done(((bf16[2048,2048]{1,0:T(8,128)(2,1)}), bf16[256,2048]{1,0:T(8,128)(2,1)}) %reduce-scatter.21.cloned.1.call-update) | async-done | bytes 1048592 | tf_op jit(solution)/shard_map/reduce_scatter | solution.py:321
  1949.4 87.4 %reduce-scatter.23.cloned.1.call-done = bf16[2048,256]{1,0:T(8,128)(2,1)} async-done(((bf16[2048,2048]{1,0:T(8,128)(2,1)}), bf16[2048,256]{1,0:T(8,128)(2,1)}) %reduce-scatter.23.cloned.1.call-update) | async-done | bytes 1048592 | tf_op jit(solution)/shard_map/reduce_scatter | solution.py:324
  2039.5 68.8 %reduce-scatter.9.cloned.1.call-done = bf16[1536,512]{1,0:T(8,128)(2,1)} async-done(((bf16[1536,2048]{1,0:T(8,128)(2,1)}), bf16[1536,512]{1,0:T(8,128)(2,1)}) %reduce-scatter.9.cloned.1.call-update) | async-done | bytes 1572880 | tf_op jit(solution)/shard_map/reduce_scatter | solution.py:300
  (361 shorter events, 440.9 us)
Async XLA Ops:
  7.2 119.0 %all-gather.11.cloned.1.call-start = ((), (), s32[]{:S(2)}) async-start(), calls=%async_computation.9 | async-start | bytes 2359296 | tf_op jit(solution)/shard_map/all_gather | solution.py:203
  7.9 124.6 %all-gather.9.cloned.1.call-start = ((), (), s32[]{:S(2)}) async-start(), calls=%async_computation.8 | async-start | bytes 2359296 | tf_op jit(solution)/shard_map/all_gather | solution.py:202
  8.7 186.8 %all-gather.13.cloned.1.call-start = ((), (), s32[]{:S(2)}) async-start(), calls=%async_computation.10 | async-start | bytes 2359296 | tf_op jit(solution)/shard_map/all_gather | solution.py:204
  9.4 241.9 %all-gather.15.cloned.1.call-start = ((), (), s32[]{:S(2)}) async-start(), calls=%async_computation.11 | async-start | bytes 2359296 | tf_op jit(solution)/shard_map/all_gather | solution.py:205
  9.4 38.6 %collective-permute-start = (bf16[1536,512]{1,0:T(8,128)(2,1)}, bf16[1536,512]{1,0:T(8,128)(2,1)S(1)}, u32[]{:S(2)}, u32[]{:S(2)}) collective-permute-start(bf16[1536,512]{1,0:T(8,128)(2,1)} %param.19), channel_id=1, source_target_pairs={{0,1},{1,2},{2,3},{3,0},{4,5},{5,6},{6,7},{7,4},{8,9},{9,10},{10,1... | collective-permute-start | bytes 4718600 | tf_op jit(solution)/shard_map/ppermute | solution.py:196
  48.0 38.3 %collective-permute-start.1 = (bf16[1536,512]{1,0:T(8,128)(2,1)S(1)}, bf16[1536,512]{1,0:T(8,128)(2,1)}, u32[]{:S(2)}, u32[]{:S(2)}) collective-permute-start(bf16[1536,512]{1,0:T(8,128)(2,1)S(1)} %collective-permute-done), channel_id=1, source_target_pairs={{0,1},{1,2},{2,3},{3,0},{4,5},{5,6},{6,7},{7,4},{8,9},{9,10},{10,1... | collective-permute-start | bytes 4718600 | tf_op jit(solution)/shard_map/ppermute | solution.py:196
  48.8 69.3 %collective-permute-start.2 = (bf16[1536,512]{1,0:T(8,128)(2,1)}, bf16[1536,512]{1,0:T(8,128)(2,1)S(1)}, u32[]{:S(2)}, u32[]{:S(2)}) collective-permute-start(bf16[1536,512]{1,0:T(8,128)(2,1)} %param.19), channel_id=1, source_target_pairs={{0,3},{1,0},{2,1},{3,2},{4,7},{5,4},{6,5},{7,6},{8,11},{9,8},{10,9... | collective-permute-start | bytes 4718600 | tf_op jit(solution)/shard_map/ppermute | solution.py:198
  51.0 450.2 %all-reduce.7.cloned.1.call-start = ((), (), s32[]{:S(2)}) async-start(), calls=%async_computation.12 | async-start | bytes 25165824 | tf_op jit(solution)/shard_map/psum | solution.py:228
  58.8 31.5 %copy-start.21 = (bf16[1536,512]{1,0:T(8,128)(2,1)S(1)}, bf16[1536,512]{1,0:T(8,128)(2,1)}, u32[]{:S(2)}) copy-start(bf16[1536,512]{1,0:T(8,128)(2,1)} %param.19) | copy-start | bytes 4718596
  132.4 24.3 %copy-start.10 = (f32[1536,512]{0,1:T(8,128)}, f32[1536,512]{0,1:T(8,128)S(1)}, u32[]{:S(2)}) copy-start(f32[1536,512]{0,1:T(8,128)S(1)} %get-tuple-element.327) | copy-start | bytes 9437188
  132.5 24.3 %copy-start.50 = (f32[512]{0:T(512)S(1)}, f32[512]{0:T(512)}, u32[]{:S(2)}) copy-start(f32[512]{0:T(512)} %param.28) | copy-start | bytes 6148
  261.5 323.3 %all-gather.17.cloned.1.call-start = ((), (), s32[]{:S(2)}) async-start(), calls=%async_computation.13 | async-start | bytes 9437184 | tf_op jit(solution)/shard_map/all_gather | solution.py:206
  262.0 404.8 %all-gather.19.cloned.1.call-start = ((), (), s32[]{:S(2)}) async-start(), calls=%async_computation.14 | async-start | bytes 9437184 | tf_op jit(solution)/shard_map/all_gather | solution.py:207
  262.8 486.7 %all-gather.21.cloned.1.call-start = ((), (), s32[]{:S(2)}) async-start(), calls=%async_computation.15 | async-start | bytes 9437184 | tf_op jit(solution)/shard_map/all_gather | solution.py:208
  263.5 243.9 %copy-start.45 = (f32[2048]{0:T(1024)S(1)}, f32[2048]{0:T(1024)}, u32[]{:S(2)}) copy-start(f32[2048]{0:T(1024)} %param.29) | copy-start | bytes 24580
  263.6 742.5 %all-reduce.9.cloned.1.call-start = ((), (), s32[]{:S(2)}) async-start(), calls=%async_computation.16 | async-start | bytes 25165824 | tf_op jit(solution)/shard_map/psum | solution.py:240
  768.4 309.2 %all-gather.23.cloned.1.call-start = ((), (), s32[]{:S(2)}) async-start(), calls=%async_computation.17 | async-start | bytes 7864320 | tf_op jit(solution)/shard_map/all_gather | solution.py:246
  769.0 308.6 %copy-start.47 = (f32[2048]{0:T(1024)S(1)}, f32[2048]{0:T(1024)}, u32[]{:S(2)}) copy-start(f32[2048]{0:T(1024)} %param.30) | copy-start | bytes 24580
  769.0 634.3 %all-reduce.11.cloned.1.call-start = ((), (), s32[]{:S(2)}) async-start(), calls=%async_computation.18 | async-start | bytes 25165824 | tf_op jit(solution)/shard_map/psum | solution.py:261
  1124.0 19.2 copy-start.54
  1163.8 621.1 %reduce-scatter.11.cloned.1.call-start = ((), (), s32[]{:S(2)}) async-start(), calls=%async_computation.20 | async-start | bytes 2359296 | tf_op jit(solution)/shard_map/reduce_scatter | solution.py:306
  1165.2 238.1 %copy-start.42 = (f32[1536]{0:T(1024)S(1)}, f32[1536]{0:T(1024)}, u32[]{:S(2)}) copy-start(f32[1536]{0:T(1024)} %copy-done.41) | copy-start | bytes 18436
  1165.2 238.1 %copy-start.46 = (f32[2048]{0:T(1024)S(1)}, f32[2048]{0:T(1024)}, u32[]{:S(2)}) copy-start(f32[2048]{0:T(1024)} %param.29) | copy-start | bytes 24580
  1490.4 13.4 slice-start
  1531.0 13.4 slice-start
  1617.9 168.9 %reduce-scatter.13.cloned.1.call-start = ((), (), s32[]{:S(2)}) async-start(), calls=%async_computation.21 | async-start | bytes 2359296 | tf_op jit(solution)/shard_map/reduce_scatter | solution.py:309
  1629.8 158.8 %reduce-scatter.15.cloned.1.call-start = ((), (), s32[]{:S(2)}) async-start(), calls=%async_computation.22 | async-start | bytes 2359296 | tf_op jit(solution)/shard_map/reduce_scatter | solution.py:312
  1639.3 151.1 %reduce-scatter.17.cloned.1.call-start = ((), (), s32[]{:S(2)}) async-start(), calls=%async_computation.23 | async-start | bytes 2359296 | tf_op jit(solution)/shard_map/reduce_scatter | solution.py:315
  1646.9 209.6 %reduce-scatter.19.cloned.1.call-start = ((), (), s32[]{:S(2)}) async-start(), calls=%async_computation.24 | async-start | bytes 9437184 | tf_op jit(solution)/shard_map/reduce_scatter | solution.py:318
  1666.4 280.3 %reduce-scatter.21.cloned.1.call-start = ((), (), s32[]{:S(2)}) async-start(), calls=%async_computation.25 | async-start | bytes 9437184 | tf_op jit(solution)/shard_map/reduce_scatter | solution.py:321
  1686.1 350.7 %reduce-scatter.23.cloned.1.call-start = ((), (), s32[]{:S(2)}) async-start(), calls=%async_computation.26 | async-start | bytes 9437184 | tf_op jit(solution)/shard_map/reduce_scatter | solution.py:324
  1706.1 402.2 %reduce-scatter.9.cloned.1.call-start = ((), (), s32[]{:S(2)}) async-start(), calls=%async_computation.19 | async-start | bytes 7864320 | tf_op jit(solution)/shard_map/reduce_scatter | solution.py:300
  (63 other events, 347.1 us)
Sparse Core Ops, SparseCore 0:
  9.6 31.8 all-gather.10
  43.1 28.5 all-gather.8
  73.3 28.5 all-gather.12
  103.3 29.9 all-gather.14
  261.6 239.5 all-reduce.6
  502.7 82.0 all-gather.16
  586.3 80.5 all-gather.18
  668.5 80.9 all-gather.20
  768.5 237.4 all-reduce.8
  1007.7 69.8 all-gather.22
  1164.0 239.2 all-reduce.10
  1618.0 36.0 reduce-scatter.10
  1657.0 34.5 reduce-scatter.12
  1694.3 34.5 reduce-scatter.14
  1731.6 34.7 reduce-scatter.16
  1768.6 87.8 reduce-scatter.18
  1858.6 87.9 reduce-scatter.20
  1948.8 87.9 reduce-scatter.22
  2039.8 68.4 reduce-scatter.8
